TPU v7x, 32 devices: a whole 2x2x4 slice. The times are simulated.
32 devices in a mesh: row: 4 (over x, core), col: 8 (over z, y).
Axes of the slice: x: 2, y: 2, z: 4, core: 2. Of those that a mesh axis runs over, the one named last changes fastest.
Arguments:
- inputs: bfloat16 [512, 8192], P('col', 'row'), may hold values from -6 to 6
- cotangent: bfloat16 [512, 8192], P('col', 'row'), may hold values from -6 to 6
- gate_pre: bfloat16 [512, 16384], P('row', 'col'), may hold values from -8 to 8
- up_pre: bfloat16 [512, 16384], P('row', 'col'), may hold values from -6 to 6
- w_gate: bfloat16 [8192, 16384], P('row', 'col'), may hold values from -0.0625 to 0.0625
- w_up: bfloat16 [8192, 16384], P('row', 'col'), may hold values from -0.0625 to 0.0625
- w_down: bfloat16 [16384, 8192], P('col', 'row'), may hold values from -0.046875 to 0.046875
Outputs:
- grad_inputs: bfloat16 [512, 8192], P('col', 'row')
- grad_gate: float32 [8192, 16384], P('row', 'col')
- grad_up: float32 [8192, 16384], P('row', 'col')
- grad_down: float32 [16384, 8192], P('col', 'row')
All inputs are finite; a program needn't handle non-finite values.
Results may differ from a plain program's by a relative error of at most 0.0049.
Values may be sent and summed in bfloat16 or wider, within the bound.
A program may use at most 128 MiB of HBM per device.

v0:
```python
import math
import jax
import jax.numpy as jnp
from jax import lax
from jax.sharding import PartitionSpec as P


def swiglu_back(gate_pre, up_pre, grad_hidden):
    gate_f = gate_pre.astype(jnp.float32)
    up_f = up_pre.astype(jnp.float32)
    sig = jax.nn.sigmoid(gate_f)
    act = gate_f * sig
    hidden = (act * up_f).astype(jnp.bfloat16)
    grad_gate_pre = (grad_hidden * up_f * sig * (1.0 + gate_f * (1.0 - sig))).astype(jnp.bfloat16)
    grad_up_pre = (grad_hidden * act).astype(jnp.bfloat16)
    return (hidden, grad_gate_pre, grad_up_pre)


def contract_last(left, right):
    return lax.dot_general(
        left, right, (((1,), (1,)), ((), ())), preferred_element_type=jnp.float32
    )


def contract_first(left, right):
    return lax.dot_general(
        left, right, (((0,), (0,)), ((), ())), preferred_element_type=jnp.float32
    )


def per_device(inputs, cotangent, gate_pre, up_pre, w_gate, w_up, w_down):
    inputs_all, cotan_all = (
        lax.all_gather(inputs, "col", axis=0, tiled=True),
        lax.all_gather(cotangent, "col", axis=0, tiled=True),
    )
    grad_hidden = lax.psum_scatter(
        contract_last(cotan_all, w_down), "row", scatter_dimension=0, tiled=True
    )
    hidden, grad_gate_pre, grad_up_pre = swiglu_back(gate_pre, up_pre, grad_hidden)
    hidden_all, gate_grad_all, up_grad_all = (
        lax.all_gather(hidden, "row", axis=0, tiled=True),
        lax.all_gather(grad_gate_pre, "row", axis=0, tiled=True),
        lax.all_gather(grad_up_pre, "row", axis=0, tiled=True),
    )
    grad_inputs = lax.psum_scatter(
        contract_last(gate_grad_all, w_gate) + contract_last(up_grad_all, w_up),
        "col",
        scatter_dimension=0,
        tiled=True,
    )
    scale = 1.0 / math.sqrt(inputs_all.shape[0])
    grad_gate = contract_first(inputs_all, gate_grad_all) * scale
    grad_up = contract_first(inputs_all, up_grad_all) * scale
    grad_down = contract_first(hidden_all, cotan_all) * scale
    return (grad_inputs.astype(jnp.bfloat16), grad_gate, grad_up, grad_down)


def solution(mesh):
    in_specs = (
        P("col", "row"),
        P("col", "row"),
        P("row", "col"),
        P("row", "col"),
        P("row", "col"),
        P("row", "col"),
        P("col", "row"),
    )
    out_specs = (P("col", "row"), P("row", "col"), P("row", "col"), P("col", "row"))
    return jax.shard_map(
        per_device, mesh=mesh, in_specs=in_specs, out_specs=out_specs, check_vma=False
    )
```

profile of v0, /device:TPU:0, one launch (start us, length us, event | category | flops | bytes accessed | tf_op | source)
XLA Modules:
  0.0 340.3 jit_solution(5187956274251306020)
XLA Ops:
  7.2 0.0 all-gather.6.cloned.1.call-start
  7.2 0.7 all-gather.6.cloned.1.call-update
  7.9 0.0 reduce-scatter.3.cloned.1.call-start
  7.9 54.0 %all-gather.6.cloned.1.call-done = bf16[512,2048]{1,0:T(8,128)(2,1)} async-done(((bf16[64,2048]{1,0:T(8,128)(2,1)}), bf16[512,2048]{1,0:T(8,128)(2,1)}) %all-gather.6.cloned.1.call-update) | async-done | bytes 2097168 | tf_op jit(solution)/shard_map/all_gather | solution.py:34
  61.9 10.6 %fusion.8 = f32[512,2048]{1,0:T(8,128)} fusion(bf16[512,2048]{1,0:T(8,128)(2,1)} %all-gather.6.cloned.1.call-done, bf16[2048,2048]{1,0:T(8,128)(2,1)} %param.13), kind=kOutput, calls=%fused_computation.18 | convolution fusion | flops 4294967296 | bytes 14680064 | tf_op jit(solution)/shard_map/dot_general | solution.py:20
  72.5 0.0 copy-start
  72.5 0.0 copy-start.1
  72.5 0.0 reduce-scatter.3.cloned.1.call-update
  72.5 0.0 all-gather.8.cloned.1.call-start
  72.6 43.2 %reduce-scatter.3.cloned.1.call-done = f32[128,2048]{1,0:T(8,128)} async-done(((f32[512,2048]{1,0:T(8,128)}), f32[128,2048]{1,0:T(8,128)}) %reduce-scatter.3.cloned.1.call-update) | async-done | bytes 1048592 | tf_op jit(solution)/shard_map/reduce_scatter | solution.py:36
  115.8 0.0 copy-done
  115.8 0.0 copy-done.1
  115.8 2.9 multiply_convert_fusion
  118.7 0.0 all-gather.8.cloned.1.call-update
  118.8 0.0 all-gather.10.cloned.1.call-start
  118.8 0.5 all-gather.10.cloned.1.call-update
  119.3 0.0 all-gather.12.cloned.1.call-start
  119.4 0.5 all-gather.12.cloned.1.call-update
  119.9 0.0 all-gather.14.cloned.1.call-start
  120.0 0.5 all-gather.14.cloned.1.call-update
  120.5 0.2 reduce-scatter.5.cloned.1.call-start
  120.7 20.7 %all-gather.8.cloned.1.call-done = bf16[512,2048]{1,0:T(8,128)(2,1)} async-done(((bf16[128,2048]{1,0:T(8,128)(2,1)}), bf16[512,2048]{1,0:T(8,128)(2,1)}) %all-gather.8.cloned.1.call-update) | async-done | bytes 2097168 | tf_op jit(solution)/shard_map/all_gather | solution.py:42
  141.5 10.6 %fusion.9 = f32[512,2048]{1,0:T(8,128)} fusion(bf16[512,2048]{1,0:T(8,128)(2,1)} %all-gather.8.cloned.1.call-done, bf16[2048,2048]{1,0:T(8,128)(2,1)} %param.11), kind=kOutput, calls=%fused_computation.19 | convolution fusion | flops 4294967296 | bytes 14680064 | tf_op jit(solution)/shard_map/dot_general | solution.py:20
  152.0 14.0 %all-gather.10.cloned.1.call-done = bf16[512,2048]{1,0:T(8,128)(2,1)} async-done(((bf16[128,2048]{1,0:T(8,128)(2,1)}), bf16[512,2048]{1,0:T(8,128)(2,1)}) %all-gather.10.cloned.1.call-update) | async-done | bytes 2097168 | tf_op jit(solution)/shard_map/all_gather | solution.py:43
  166.1 11.6 %convolution_add_fusion = f32[512,2048]{1,0:T(8,128)} fusion(f32[512,2048]{1,0:T(8,128)} %fusion.9, bf16[512,2048]{1,0:T(8,128)(2,1)} %all-gather.10.cloned.1.call-done, bf16[2048,2048]{1,0:T(8,128)(2,1)} %param.12), kind=kOutput, calls=%fused_computation.3 | convolution fusion | flops 4296015872 | bytes 18874368 | tf_op jit(solution)/shard_map/dot_general | solution.py:20
  177.7 0.0 copy-start.3
  177.7 0.0 reduce-scatter.5.cloned.1.call-update
  177.7 39.4 %all-gather.12.cloned.1.call-done = bf16[512,2048]{1,0:T(8,128)(2,1)} async-done(((bf16[64,2048]{1,0:T(8,128)(2,1)}), bf16[512,2048]{1,0:T(8,128)(2,1)}) %all-gather.12.cloned.1.call-update) | async-done | bytes 2097168 | tf_op jit(solution)/shard_map/all_gather | solution.py:33
  217.2 0.0 copy-done.3
  217.2 10.1 %multiply_bitcast_fusion.1 = f32[2048,2048]{0,1:T(8,128)} fusion(bf16[512,2048]{1,0:T(8,128)(2,1)S(1)} %copy-done.3, bf16[512,2048]{1,0:T(8,128)(2,1)} %all-gather.12.cloned.1.call-done), kind=kOutput, calls=%fused_computation.1 | convolution fusion | flops 4299161600 | bytes 20971520 | tf_op jit(solution)/shard_map/dot_general | solution.py:26
  227.3 0.0 copy-start.4
  227.3 17.8 %copy.11 = f32[2048,2048]{1,0:T(8,128)} copy(f32[2048,2048]{0,1:T(8,128)} %multiply_bitcast_fusion.1) | data formatting | bytes 33554432
  245.1 0.0 copy-done.4
  245.1 10.1 %multiply_bitcast_fusion = f32[2048,2048]{0,1:T(8,128)} fusion(bf16[512,2048]{1,0:T(8,128)(2,1)S(1)} %copy-done.4, bf16[512,2048]{1,0:T(8,128)(2,1)} %all-gather.12.cloned.1.call-done), kind=kOutput, calls=%fused_computation | convolution fusion | flops 4299161600 | bytes 20971520 | tf_op jit(solution)/shard_map/dot_general | solution.py:26
  255.2 0.0 copy-start.2
  255.2 17.9 %copy.12 = f32[2048,2048]{1,0:T(8,128)} copy(f32[2048,2048]{0,1:T(8,128)} %multiply_bitcast_fusion) | data formatting | bytes 33554432
  273.1 0.0 all-gather.14.cloned.1.call-done
  273.1 0.0 copy-done.2
  273.1 10.2 %convolution_multiply_fusion = f32[2048,2048]{1,0:T(8,128)} fusion(bf16[512,2048]{1,0:T(8,128)(2,1)} %all-gather.14.cloned.1.call-done, bf16[512,2048]{1,0:T(8,128)(2,1)S(1)} %copy-done.2), kind=kOutput, calls=%fused_computation.2 | convolution fusion | flops 4299161600 | bytes 20971520 | tf_op jit(solution)/shard_map/dot_general | solution.py:26
  283.2 48.4 %reduce-scatter.5.cloned.1.call-done = f32[64,2048]{1,0:T(8,128)} async-done(((f32[512,2048]{1,0:T(8,128)}), f32[64,2048]{1,0:T(8,128)}) %reduce-scatter.5.cloned.1.call-update) | async-done | bytes 524304 | tf_op jit(solution)/shard_map/reduce_scatter | solution.py:45
  331.7 1.8 convert_element_type.22
Async XLA Ops:
  7.2 54.8 %all-gather.6.cloned.1.call-start = ((), (), s32[]{:S(2)}) async-start(), calls=%async_computation.2 | async-start | bytes 2359296 | tf_op jit(solution)/shard_map/all_gather | solution.py:34
  7.9 107.9 %reduce-scatter.3.cloned.1.call-start = ((), (), s32[]{:S(2)}) async-start(), calls=%async_computation.3 | async-start | bytes 5242880 | tf_op jit(solution)/shard_map/reduce_scatter | solution.py:36
  72.5 43.3 %copy-start = (bf16[128,2048]{1,0:T(8,128)(2,1)S(1)}, bf16[128,2048]{1,0:T(8,128)(2,1)}, u32[]{:S(2)}) copy-start(bf16[128,2048]{1,0:T(8,128)(2,1)} %param.9) | copy-start | bytes 1572868
  72.5 43.3 %copy-start.1 = (bf16[128,2048]{1,0:T(8,128)(2,1)S(1)}, bf16[128,2048]{1,0:T(8,128)(2,1)}, u32[]{:S(2)}) copy-start(bf16[128,2048]{1,0:T(8,128)(2,1)} %param.10) | copy-start | bytes 1572868
  72.5 68.9 %all-gather.8.cloned.1.call-start = ((), (), s32[]{:S(2)}) async-start(), calls=%async_computation.4 | async-start | bytes 2621440 | tf_op jit(solution)/shard_map/all_gather | solution.py:42
  118.8 47.3 %all-gather.10.cloned.1.call-start = ((), (), s32[]{:S(2)}) async-start(), calls=%async_computation.5 | async-start | bytes 2621440 | tf_op jit(solution)/shard_map/all_gather | solution.py:43
  119.3 97.8 %all-gather.12.cloned.1.call-start = ((), (), s32[]{:S(2)}) async-start(), calls=%async_computation.7 | async-start | bytes 2359296 | tf_op jit(solution)/shard_map/all_gather | solution.py:33
  119.9 153.2 %all-gather.14.cloned.1.call-start = ((), (), s32[]{:S(2)}) async-start(), calls=%async_computation.8 | async-start | bytes 2621440 | tf_op jit(solution)/shard_map/all_gather | solution.py:41
  120.5 211.2 %reduce-scatter.5.cloned.1.call-start = ((), (), s32[]{:S(2)}) async-start(), calls=%async_computation.6 | async-start | bytes 4718592 | tf_op jit(solution)/shard_map/reduce_scatter | solution.py:45
  177.7 39.5 %copy-start.3 = (bf16[512,2048]{1,0:T(8,128)(2,1)S(1)}, bf16[512,2048]{1,0:T(8,128)(2,1)}, u32[]{:S(2)}) copy-start(bf16[512,2048]{1,0:T(8,128)(2,1)} %all-gather.8.cloned.1.call-done) | copy-start | bytes 6291460
  227.3 17.8 %copy-start.4 = (bf16[512,2048]{1,0:T(8,128)(2,1)S(1)}, bf16[512,2048]{1,0:T(8,128)(2,1)}, u32[]{:S(2)}) copy-start(bf16[512,2048]{1,0:T(8,128)(2,1)} %all-gather.10.cloned.1.call-done) | copy-start | bytes 6291460
  255.2 17.9 %copy-start.2 = (bf16[512,2048]{1,0:T(8,128)(2,1)S(1)}, bf16[512,2048]{1,0:T(8,128)(2,1)}, u32[]{:S(2)}) copy-start(bf16[512,2048]{1,0:T(8,128)(2,1)} %all-gather.6.cloned.1.call-done) | copy-start | bytes 6291460
Sparse Core Ops, SparseCore 0:
  10.1 51.7 all-gather.5
  72.7 43.1 reduce-scatter.2
  118.9 22.5 all-gather.7
  143.5 22.5 all-gather.9
  168.0 49.0 all-gather.11
  218.6 21.0 all-gather.13
  243.3 88.2 reduce-scatter.4
where the time goes:
time: 341 us; the launch traced here: 340 us
  waiting for transfers between devices  222 us (65%)
  matrix products  63.2 us (19%)
  local copies, waits for them, and re-layouts  35.6 us (10%)
  between operations  14.1 us (4%)
  other arithmetic  4.69 us (1%)
    all_gather x1, waiting for transfers between devices, per_device(): lax.all_gather(cotangent, 'col', axis=0, tiled=True)  54 us
    reduce_scatter x1, waiting for transfers between devices, per_device(): lax.psum_scatter(contract_last(gate_grad_all, w_gate) + contract_last(up_...  48.4 us
    reduce_scatter x1, waiting for transfers between devices, per_device(): lax.psum_scatter(contract_last(cotan_all, w_down), 'row', scatter_dimensi...  43.2 us
    all_gather x1, waiting for transfers between devices, per_device(): lax.all_gather(inputs, 'col', axis=0, tiled=True)  39.4 us
    unnamed x12, local copies, waits for them, and re-layouts  35.6 us
    dot_general x3, matrix products, contract_last(): lax.dot_general(left, right, (((1,), (1,)), ((), ())), preferred_element_...  32.8 us
    dot_general x3, matrix products, contract_first(): lax.dot_general(left, right, (((0,), (0,)), ((), ())), preferred_element_...  30.4 us
    all_gather x1, waiting for transfers between devices, per_device(): lax.all_gather(grad_gate_pre, 'row', axis=0, tiled=True)  20.7 us
  transfers between devices with their start and end apart: 7, of which 6 were waited for; matrix products, arithmetic and copies ran while one was open for 26% of the time, Pallas kernels for 0%

commit v1 on v0

--- a/solution.py
+++ b/solution.py
@@ -3,6 +3,13 @@
 import jax.numpy as jnp
 from jax import lax
 from jax.sharding import PartitionSpec as P
+
+
+def swapped_in(x, name, dim):
+    peers = lax.axis_size(name)
+    parts = jnp.stack([x for _ in range(peers)])
+    parts = lax.all_to_all(parts, name, split_axis=0, concat_axis=0)
+    return jnp.concatenate(parts, axis=dim)
 
 
 def swiglu_back(gate_pre, up_pre, grad_hidden):
@@ -30,7 +37,7 @@
 
 def per_device(inputs, cotangent, gate_pre, up_pre, w_gate, w_up, w_down):
     inputs_all, cotan_all = (
-        lax.all_gather(inputs, "col", axis=0, tiled=True),
+        swapped_in(inputs, "col", 0),
         lax.all_gather(cotangent, "col", axis=0, tiled=True),
     )
     grad_hidden = lax.psum_scatter(

time: 341 us -> 340 us (level)
  waiting for transfers between devices: 222 us -> 134 us
  blocking collectives: 0 us -> 87.7 us
    all_to_all x0 -> x1, blocking collectives: none -> 87.7 us  [swapped_in(): parts = lax.all_to_all(parts, name, split_axis=0, concat_axis=0)]
    reduce_scatter x1, waiting for transfers between devices: 48.4 us -> 0.01 us  [per_device(): lax.psum_scatter(contract_last(gate_grad_all, w_gate) + contract_last(up_...]
    all_gather x1 -> x0, waiting for transfers between devices: 39.4 us -> none  [per_device(): lax.all_gather(inputs, 'col', axis=0, tiled=True)]
  transfers between devices with their start and end apart: 7 -> 6, of which waited for: 6 -> 4; matrix products, arithmetic and copies ran while one was open for 26% -> 26% of each run, Pallas kernels for 0% -> 0%
where the time goes in v1:
time: 340 us
  waiting for transfers between devices  134 us (39%)
  blocking collectives  87.7 us (26%)
  matrix products  61.6 us (18%)
  local copies, waits for them, and re-layouts  36.6 us (11%)
  between operations  14.1 us (4%)
  other arithmetic  4.72 us (1%)
    all_to_all x1, blocking collectives, swapped_in(): parts = lax.all_to_all(parts, name, split_axis=0, concat_axis=0)  87.7 us
    all_gather x1, waiting for transfers between devices, per_device(): lax.all_gather(cotangent, 'col', axis=0, tiled=True)  54 us
    reduce_scatter x1, waiting for transfers between devices, per_device(): lax.psum_scatter(contract_last(cotan_all, w_down), 'row', scatter_dimensi...  43.2 us
    unnamed x12, local copies, waits for them, and re-layouts  36.4 us
    dot_general x3, matrix products, contract_last(): lax.dot_general(left, right, (((1,), (1,)), ((), ())), preferred_element_...  32.8 us
    dot_general x3, matrix products, contract_first(): lax.dot_general(left, right, (((0,), (0,)), ((), ())), preferred_element_...  28.8 us
    all_gather x1, waiting for transfers between devices, per_device(): lax.all_gather(grad_gate_pre, 'row', axis=0, tiled=True)  21.3 us
    all_gather x1, waiting for transfers between devices, per_device(): lax.all_gather(grad_up_pre, 'row', axis=0, tiled=True)  14 us
  transfers between devices with their start and end apart: 6, of which 4 were waited for; matrix products, arithmetic and copies ran while one was open for 26% of the time, Pallas kernels for 0%

profile of v1, /device:TPU:0, one launch (start us, length us, event | category | flops | bytes accessed | tf_op | source)
XLA Modules:
  0.0 339.6 jit_solution(10721222945920521104)
XLA Ops:
  7.2 0.0 all-gather.5.cloned.1.call-start
  7.2 0.7 all-gather.5.cloned.1.call-update
  7.9 0.0 reduce-scatter.3.cloned.1.call-start
  7.9 54.0 %all-gather.5.cloned.1.call-done = bf16[512,2048]{1,0:T(8,128)(2,1)} async-done(((bf16[64,2048]{1,0:T(8,128)(2,1)}), bf16[512,2048]{1,0:T(8,128)(2,1)}) %all-gather.5.cloned.1.call-update) | async-done | bytes 2097168 | tf_op jit(solution)/shard_map/all_gather | solution.py:41
  61.9 10.6 %fusion.8 = f32[512,2048]{1,0:T(8,128)} fusion(bf16[512,2048]{1,0:T(8,128)(2,1)} %all-gather.5.cloned.1.call-done, bf16[2048,2048]{1,0:T(8,128)(2,1)} %param.13), kind=kOutput, calls=%fused_computation.18 | convolution fusion | flops 4294967296 | bytes 14680064 | tf_op jit(solution)/shard_map/dot_general | solution.py:27
  72.5 0.0 copy-start
  72.5 0.0 copy-start.1
  72.5 0.0 reduce-scatter.3.cloned.1.call-update
  72.5 0.0 all-gather.7.cloned.1.call-start
  72.6 43.2 %reduce-scatter.3.cloned.1.call-done = f32[128,2048]{1,0:T(8,128)} async-done(((f32[512,2048]{1,0:T(8,128)}), f32[128,2048]{1,0:T(8,128)}) %reduce-scatter.3.cloned.1.call-update) | async-done | bytes 1048592 | tf_op jit(solution)/shard_map/reduce_scatter | solution.py:43
  115.8 0.0 copy-done
  115.8 0.0 copy-done.1
  115.8 2.9 multiply_convert_fusion
  118.8 0.0 all-gather.7.cloned.1.call-update
  118.8 0.0 all-gather.9.cloned.1.call-start
  118.8 0.5 all-gather.9.cloned.1.call-update
  119.4 0.0 all-gather.11.cloned.1.call-start
  119.4 0.5 all-gather.11.cloned.1.call-update
  119.9 0.2 reduce-scatter.5.cloned.1.call-start
  120.2 21.3 %all-gather.7.cloned.1.call-done = bf16[512,2048]{1,0:T(8,128)(2,1)} async-done(((bf16[128,2048]{1,0:T(8,128)(2,1)}), bf16[512,2048]{1,0:T(8,128)(2,1)}) %all-gather.7.cloned.1.call-update) | async-done | bytes 2097168 | tf_op jit(solution)/shard_map/all_gather | solution.py:49
  141.5 10.6 %fusion.9 = f32[512,2048]{1,0:T(8,128)} fusion(bf16[512,2048]{1,0:T(8,128)(2,1)} %all-gather.7.cloned.1.call-done, bf16[2048,2048]{1,0:T(8,128)(2,1)} %param.11), kind=kOutput, calls=%fused_computation.19 | convolution fusion | flops 4294967296 | bytes 14680064 | tf_op jit(solution)/shard_map/dot_general | solution.py:27
  152.1 14.0 %all-gather.9.cloned.1.call-done = bf16[512,2048]{1,0:T(8,128)(2,1)} async-done(((bf16[128,2048]{1,0:T(8,128)(2,1)}), bf16[512,2048]{1,0:T(8,128)(2,1)}) %all-gather.9.cloned.1.call-update) | async-done | bytes 2097168 | tf_op jit(solution)/shard_map/all_gather | solution.py:50
  166.1 11.7 %convolution_add_fusion = f32[512,2048]{1,0:T(8,128)} fusion(f32[512,2048]{1,0:T(8,128)} %fusion.9, bf16[512,2048]{1,0:T(8,128)(2,1)} %all-gather.9.cloned.1.call-done, bf16[2048,2048]{1,0:T(8,128)(2,1)} %param.12), kind=kOutput, calls=%fused_computation.3 | convolution fusion | flops 4296015872 | bytes 18874368 | tf_op jit(solution)/shard_map/dot_general | solution.py:27
  177.7 0.0 copy-start.2
  177.7 0.0 reduce-scatter.5.cloned.1.call-update
  177.8 0.9 copy-done.2
  178.7 0.0 copy-start.4
  178.7 0.2 stack.2
  178.9 87.7 %all_to_all.5 = bf16[8,64,2048]{2,1,0:T(8,128)(2,1)S(1)} all-to-all(bf16[8,64,2048]{2,1,0:T(8,128)(2,1)S(1)} %stack.2), channel_id=1, replica_groups=mesh['row'=4,'col'=8] {'col'}, dimensions={0} | all-to-all | bytes 4194304 | tf_op jit(solution)/shard_map/all_to_all | solution.py:11
  266.7 0.0 copy-done.4
  266.7 8.6 %multiply_bitcast_fusion.1 = f32[2048,2048]{0,1:T(8,128)} fusion(bf16[512,2048]{1,0:T(8,128)(2,1)S(1)} %copy-done.4, bf16[512,2048]{1,0:T(8,128)(2,1)S(1)} %bitcast.17), kind=kOutput, calls=%fused_computation.1 | convolution fusion | flops 4299161600 | bytes 20971520 | tf_op jit(solution)/shard_map/dot_general | solution.py:33
  275.3 17.7 %copy.11 = f32[2048,2048]{1,0:T(8,128)} copy(f32[2048,2048]{0,1:T(8,128)} %multiply_bitcast_fusion.1) | data formatting | bytes 33554432
  292.9 10.1 %multiply_bitcast_fusion = f32[2048,2048]{0,1:T(8,128)} fusion(bf16[512,2048]{1,0:T(8,128)(2,1)} %all-gather.9.cloned.1.call-done, bf16[512,2048]{1,0:T(8,128)(2,1)S(1)} %bitcast.18), kind=kOutput, calls=%fused_computation | convolution fusion | flops 4299161600 | bytes 20971520 | tf_op jit(solution)/shard_map/dot_general | solution.py:33
  303.0 0.0 copy-start.3
  303.1 17.8 %copy.12 = f32[2048,2048]{1,0:T(8,128)} copy(f32[2048,2048]{0,1:T(8,128)} %multiply_bitcast_fusion) | data formatting | bytes 33554432
  320.8 0.0 all-gather.11.cloned.1.call-done
  320.8 0.0 copy-done.3
  320.8 10.1 %convolution_multiply_fusion = f32[2048,2048]{1,0:T(8,128)} fusion(bf16[512,2048]{1,0:T(8,128)(2,1)} %all-gather.11.cloned.1.call-done, bf16[512,2048]{1,0:T(8,128)(2,1)S(1)} %copy-done.3), kind=kOutput, calls=%fused_computation.2 | convolution fusion | flops 4299161600 | bytes 20971520 | tf_op jit(solution)/shard_map/dot_general | solution.py:33
  331.0 0.0 reduce-scatter.5.cloned.1.call-done
  331.0 1.8 convert_element_type.22
Async XLA Ops:
  7.2 54.8 %all-gather.5.cloned.1.call-start = ((), (), s32[]{:S(2)}) async-start(), calls=%async_computation.3 | async-start | bytes 2359296 | tf_op jit(solution)/shard_map/all_gather | solution.py:41
  7.9 107.9 %reduce-scatter.3.cloned.1.call-start = ((), (), s32[]{:S(2)}) async-start(), calls=%async_computation.4 | async-start | bytes 5242880 | tf_op jit(solution)/shard_map/reduce_scatter | solution.py:43
  72.5 43.3 %copy-start = (bf16[128,2048]{1,0:T(8,128)(2,1)S(1)}, bf16[128,2048]{1,0:T(8,128)(2,1)}, u32[]{:S(2)}) copy-start(bf16[128,2048]{1,0:T(8,128)(2,1)} %param.9) | copy-start | bytes 1572868
  72.5 43.3 %copy-start.1 = (bf16[128,2048]{1,0:T(8,128)(2,1)S(1)}, bf16[128,2048]{1,0:T(8,128)(2,1)}, u32[]{:S(2)}) copy-start(bf16[128,2048]{1,0:T(8,128)(2,1)} %param.10) | copy-start | bytes 1572868
  72.5 69.0 %all-gather.7.cloned.1.call-start = ((), (), s32[]{:S(2)}) async-start(), calls=%async_computation.5 | async-start | bytes 2621440 | tf_op jit(solution)/shard_map/all_gather | solution.py:49
  118.8 47.3 %all-gather.9.cloned.1.call-start = ((), (), s32[]{:S(2)}) async-start(), calls=%async_computation.6 | async-start | bytes 2621440 | tf_op jit(solution)/shard_map/all_gather | solution.py:50
  119.4 201.5 %all-gather.11.cloned.1.call-start = ((), (), s32[]{:S(2)}) async-start(), calls=%async_computation.8 | async-start | bytes 2621440 | tf_op jit(solution)/shard_map/all_gather | solution.py:48
  119.9 211.0 %reduce-scatter.5.cloned.1.call-start = ((), (), s32[]{:S(2)}) async-start(), calls=%async_computation.7 | async-start | bytes 4718592 | tf_op jit(solution)/shard_map/reduce_scatter | solution.py:52
  177.7 0.9 copy-start.2
  178.7 88.0 %copy-start.4 = (bf16[512,2048]{1,0:T(8,128)(2,1)S(1)}, bf16[512,2048]{1,0:T(8,128)(2,1)}, u32[]{:S(2)}) copy-start(bf16[512,2048]{1,0:T(8,128)(2,1)} %all-gather.7.cloned.1.call-done) | copy-start | bytes 6291460
  303.0 17.8 %copy-start.3 = (bf16[512,2048]{1,0:T(8,128)(2,1)S(1)}, bf16[512,2048]{1,0:T(8,128)(2,1)}, u32[]{:S(2)}) copy-start(bf16[512,2048]{1,0:T(8,128)(2,1)} %all-gather.5.cloned.1.call-done) | copy-start | bytes 6291460
Sparse Core Ops, SparseCore 0:
  10.1 51.7 all-gather.4
  72.7 43.1 reduce-scatter.2
  118.9 22.5 all-gather.6
  143.5 22.5 all-gather.8
  167.5 22.5 all-gather.10
  193.6 116.0 reduce-scatter.4
